TPU v7x, 32 devices: a whole 2x2x4 slice. The times are simulated.
32 devices in a mesh: grp: 2 (over x), aux: 16 (over z, y, core).
Axes of the slice: x: 2, y: 2, z: 4, core: 2. Of those that a mesh axis runs over, the one named last changes fastest.
Arguments:
- three_index: bfloat16 [64, 256, 256], P('aux'), may hold values from -0.375 to 0.375
- relaxed: bfloat16 [512, 256], P('grp'), parts along dimension 0, may hold values from -0.375 to 0.375
- plus_amplitude: bfloat16 [512, 256], P('grp'), parts along dimension 0, may hold values from -0.375 to 0.375
- minus_amplitude: bfloat16 [512, 256], P('grp'), parts along dimension 0, may hold values from -0.375 to 0.375
- ground: bfloat16 [256, 256], replicated, may hold values from -0.375 to 0.375
- integral_grad: bfloat16 [3, 64, 512, 256], P(None, None, 'aux'), may hold values from -0.09375 to 0.09375
- metric_grad: bfloat16 [3, 64, 64], P(None, 'aux'), may hold values from -0.5 to 0.5
- function_atom: int32 [256], replicated, may hold values from 0 to 31, never falling along the last dimension, each value on 1 to 16 neighbouring positions
- aux_center: int32 [64], P('aux'), may hold values from 0 to 31, never falling along the last dimension, each value on 1 to 4 neighbouring positions
- block_list: int32 [512], replicated, may hold values from 0 to 255, as said below
- block_count: int32 [16], replicated, may hold values from 0 to 32, as said below
Outputs:
- gradient: float32 [3, 64], P(None, 'grp'), parts along dimension 1
There are 2 independent parts, one for each index of `grp`. A program takes and returns all parts, laid end to end along the dimension named above; an argument that names none is the same for every part. Nothing has to cross between parts.
Inputs may be any that keep to these rules, and one draw needn't show every extreme that they name: block_count[d] is the number of live slots of owner d; the counts sum to 256, and at least one owner has 32. `block_list`: slot s of owner d is entry d * 32 + s and is live when s < block_count[d]; each tile pair i * 16 + j is held by exactly one live slot; slots that are not live hold arbitrary tile pairs.
All inputs are finite; a program needn't handle non-finite values.
Results may differ from a plain program's by a relative error of at most 0.0032.
Values may be sent and summed in bfloat16 or wider, within the bound.
No kernel may reach another device: no remote copies, remote signals or barrier semaphores. Data moves between devices by JAX's collectives and lax.ppermute only.
A program may use at most 64 MiB of HBM per device.

v0:
```python
import jax
import jax.numpy as jnp
from jax import lax
from jax.sharding import PartitionSpec as P

TILE = 16
NATOM = 32


def on_device(
    three_index,
    relaxed,
    plus_amplitude,
    minus_amplitude,
    ground,
    integral_grad,
    metric_grad,
    function_atom,
    aux_center,
    block_list,
    block_count,
):
    highest = lax.Precision.HIGHEST
    aux_local = three_index.shape[0]
    basis_count = three_index.shape[1]
    tile_count = basis_count // TILE
    slot_depth = integral_grad.shape[2]
    slot_total = block_list.shape[0]
    fitted = jnp.einsum("pab,ab->p", three_index, relaxed, preferred_element_type=jnp.float32)
    stacked = jnp.concatenate([plus_amplitude, minus_amplitude, ground], 0)
    halves = jnp.einsum(
        "ab,pbc->pac", stacked, three_index, preferred_element_type=jnp.float32
    ).astype(jnp.bfloat16)
    paired_half = halves[:, : 2 * basis_count].reshape(aux_local, 2, basis_count, basis_count)
    paired_half = jnp.concatenate([paired_half[:, 0], paired_half[:, 1]], axis=2)
    ground_half = halves[:, 2 * basis_count :]
    partners = jnp.concatenate([plus_amplitude, -minus_amplitude], axis=1)
    exchange_part = jnp.einsum(
        "pab,cb->pac", paired_half, partners, preferred_element_type=jnp.float32
    )
    crossed = jnp.einsum("pab,bc->pac", ground_half, relaxed, preferred_element_type=jnp.float32)
    triple = (
        fitted[:, None, None] * relaxed.astype(jnp.float32)[None]
        + exchange_part
        + crossed
        + jnp.swapaxes(crossed, 1, 2)
    )
    triple = triple.astype(jnp.bfloat16)
    blocked = triple.reshape(aux_local, tile_count, TILE, tile_count, TILE).transpose(0, 1, 3, 2, 4)
    blocked = blocked.reshape(aux_local, tile_count * tile_count, TILE * TILE)
    chosen = jnp.take(blocked, block_list, axis=1)
    slot_ids = jnp.arange(slot_total, dtype=jnp.int32)
    live_mask = (slot_ids % slot_depth < block_count[slot_ids // slot_depth]).astype(jnp.float32)
    arrived = lax.all_to_all(chosen, "aux", split_axis=1, concat_axis=0, tiled=True)
    first_slot = lax.axis_index("aux") * slot_depth
    tile_ids = lax.dynamic_slice_in_dim(block_list, first_slot, slot_depth)
    slot_mask = lax.dynamic_slice_in_dim(live_mask, first_slot, slot_depth)
    contracted = jnp.einsum(
        "pgf,kpgf->kgf", arrived, integral_grad, preferred_element_type=jnp.float32
    )
    slot_count = tile_ids.shape[0]
    row_sums = contracted.reshape(3, slot_count, TILE, TILE).sum(axis=3) * slot_mask[None, :, None]
    function_ids = (tile_ids // tile_count)[:, None] * TILE + jnp.arange(TILE, dtype=jnp.int32)[
        None, :
    ]
    atom_table = (
        function_atom[function_ids][:, :, None] == jnp.arange(NATOM, dtype=jnp.int32)[None, None, :]
    ).astype(jnp.float32)
    three_part = 2.0 * jnp.einsum("kgm,gma->ka", row_sums, atom_table, precision=highest)
    all_fitted = lax.all_gather(fitted, "aux", axis=0, tiled=True)
    coupling = jnp.einsum(
        "kpq,q->kp", metric_grad.astype(jnp.float32), all_fitted, precision=highest
    )
    aux_table = (aux_center[:, None] == jnp.arange(NATOM, dtype=jnp.int32)[None, :]).astype(
        jnp.float32
    )
    metric_part = jnp.einsum("kp,pa->ka", coupling * fitted[None, :], aux_table, precision=highest)
    return lax.psum(three_part - metric_part, "aux")


def solution(mesh):
    in_specs = (
        P("aux", None, None),
        P("grp", None),
        P("grp", None),
        P("grp", None),
        P(),
        P(None, None, "aux", None),
        P(None, "aux", None),
        P(),
        P("aux"),
        P(),
        P(),
    )
    out_specs = P(None, "grp")
    return jax.shard_map(
        on_device, mesh=mesh, in_specs=in_specs, out_specs=out_specs, check_vma=False
    )
```

profile of v0, /device:TPU:0, one launch (start us, length us, event | category | flops | bytes accessed | tf_op | source)
XLA Modules:
  0.0 119.7 jit_solution(17670021363365028496)
XLA Ops:
  0.0 1.8 %fusion = bf16[4,768,256]{2,1,0:T(8,128)(2,1)S(1)} fusion(bf16[4,256,256]{2,1,0:T(8,128)(2,1)} %param.11, bf16[256,256]{1,0:T(8,128)(2,1)} %param.15, bf16[256,256]{1,0:T(8,128)(2,1)} %param.14, bf16[256,256]{1,0:T(8,128)(2,1)} %param.13), kind=kOutput, calls=%fused_computation.5 | convolution fusion | flops 404619264 | bytes 2490368 | tf_op jit(solution)/shard_map/ab,pbc->pac/dot_general | solution.py:31
  2.0 0.3 fusion.8
  2.3 0.5 copy-done.6
  2.8 0.7 neg.3
  3.5 0.9 slice_bitcast_fusion.1
  4.3 0.3 copy.42
  4.7 1.9 %convolution_bitcast_fusion.1 = f32[4]{0:T(128)S(1)} fusion(bf16[4,256,256]{2,1,0:T(8,128)(2,1)S(1)} %copy-done.4, bf16[256,256,1]{1,0,2:T(8,128)(2,1)} %bitcast.80), kind=kOutput, calls=%fused_computation.13 | convolution fusion | flops 524288 | bytes 655376 | tf_op jit(solution)/shard_map/pab,ab->p/dot_general | solution.py:29
  6.6 0.5 copy-done.11
  7.1 0.5 fusion.3
  7.6 4.2 %reshape.108 = bf16[4,16,16,16,16]{4,3,2,1,0:T(8,128)(2,1)} reshape(bf16[4,256,256]{2,1,0:T(8,128)(2,1)S(1)} %fusion.3) | data formatting | bytes 1048576 | tf_op jit(solution)/shard_map/reshape | solution.py:49
  11.7 5.2 %copy.74 = bf16[4,16,16,16,16]{4,2,3,1,0:T(8,128)(2,1)} copy(bf16[4,16,16,16,16]{4,3,2,1,0:T(8,128)(2,1)} %reshape.108) | data formatting | bytes 1048576 | tf_op jit(solution)/shard_map/reshape | solution.py:49
  17.0 5.5 %reshape.109 = bf16[4,256,256]{2,1,0:T(8,128)(2,1)S(1)} reshape(bf16[4,16,16,16,16]{4,3,2,1,0:T(8,128)(2,1)} %bitcast.77) | data formatting | bytes 1048576 | tf_op jit(solution)/shard_map/reshape | solution.py:50
  22.5 0.4 copy.44
  22.9 2.4 %gather_fusion = bf16[512,4,256]{2,1,0:T(4,128)(2,1)S(1)} fusion(bf16[4,256,256]{2,0,1:T(4,128)(2,1)S(1)} %copy.44, s32[1024]{0:T(1024)S(1)} %pad_clamp_fusion.1), kind=kCustom, calls=%fused_computation | custom fusion | bytes 2099200 | tf_op jit(solution)/shard_map/jit(_take)/gather | solution.py:51
  25.3 2.7 %select_bitcast_fusion = bf16[4,512,256]{2,0,1:T(4,128)(2,1)} fusion(bf16[512,4,256]{2,1,0:T(4,128)(2,1)S(1)} %gather_fusion, pred[512]{0:T(512)(128)(4,1)S(1)} %compare_and_fusion), kind=kLoop, calls=%fused_computation.18 | loop fusion | flops 524288 | bytes 2097664 | tf_op jit(solution)/shard_map/jit(_take)/select_n | solution.py:51
  28.0 7.4 %all-to-all-start = ((bf16[4,512,256]{2,0,1:T(4,128)(2,1)}), bf16[4,512,256]{2,0,1:T(4,128)(2,1)S(1)}, u32[]{:S(2)}, u32[]{:S(2)}) async-start(bf16[4,512,256]{2,0,1:T(4,128)(2,1)} %select_bitcast_fusion), calls=%async_computation | async-start | bytes 2097152 | tf_op jit(solution)/shard_map/all_to_all | solution.py:54
  35.7 0.7 fusion.34
  36.5 4.3 %compare_select_fusion.2 = s32[512,1]{0,1:T(1,128)S(1)} fusion(s32[]{:T(128)} %bitcast.30, s32[]{:T(128)} %bitcast.31, s32[]{:T(128)} %bitcast.32, s32[]{:T(128)} %bitcast.33, s32[]{:T(128)} %bitcast.34, s32[]{:T(128)} %bitcast.36, s32[]{:T(128)} %bitcast.35), kind=kLoop, calls=%fused_computation.49 | loop fusion | flops 11776 | bytes 2076 | tf_op jit(solution)/shard_map/gather | solution.py:53
  40.8 5.7 %fusion.25 = f32[512]{0:T(512)S(1)} fusion(pred[512]{0:T(512)(128)(4,1)S(1)} %compare_reduce_fusion, pred[512]{0:T(512)(128)(4,1)S(1)} %compare_reduce_fusion.1, pred[512]{0:T(512)(128)(4,1)S(1)} %compare_reduce_fusion.2, pred[512]{0:T(512)(128)(4,1)S(1)} %compare_reduce_fusion.3, pred[512]{0:T(512)(128)(4,1)S(1)} %compare_reduce_fusion.4, ...), kind=kLoop, calls=%fused_computation.73 | loop fusion | flops 8704 | bytes 8740 | tf_op jit(solution)/shard_map/convert_element_type | solution.py:53
  46.8 3.5 %gather_fusion.1 = s32[512]{0:T(512)S(1)} fusion(s32[256]{0:T(256)S(1)} %copy-done.1, s32[1024]{0:T(1024)S(1)} %pad_clamp_fusion), kind=kCustom, calls=%fused_computation.1 | custom fusion | bytes 6144 | tf_op jit(solution)/shard_map/gather | solution.py:67
  50.5 0.6 dynamic-slice
  51.7 0.2 dynamic-update-slice
  52.0 33.9 %all-reduce = f32[64]{0:T(128)S(1)} all-reduce(f32[64]{0:T(128)S(1)} %dynamic-update-slice), channel_id=1, replica_groups=mesh['grp'=2,'aux'=16] {'aux'}, use_global_device_ids=true, to_apply=%add | all-reduce | flops 64 | bytes 512
  85.9 0.1 fusion.29
  86.1 0.2 copy.59
  86.3 0.3 bitcast_convert_fusion
  86.6 1.5 %copy-done.2 = bf16[3,64,32,256]{3,2,1,0:T(8,128)(2,1)S(1)} copy-done((bf16[3,64,32,256]{3,2,1,0:T(8,128)(2,1)S(1)}, bf16[3,64,32,256]{3,2,1,0:T(8,128)(2,1)}, u32[]{:S(2)}) %copy-start.2) | copy-done | bytes 3145752
  88.2 0.7 multiply_reduce_fusion
  88.9 0.2 copy.57
  89.2 0.3 fusion.4
  89.5 0.2 convolution_subtract_fusion
  89.7 30.1 %psum.7 = f32[3,32]{1,0:T(4,128)} all-reduce(f32[3,32]{1,0:T(4,128)S(1)} %convolution_subtract_fusion), channel_id=1, replica_groups=mesh['grp'=2,'aux'=16] {'aux'}, use_global_device_ids=true, to_apply=%region_1.2 | all-reduce | flops 96 | bytes 768 | tf_op jit(solution)/shard_map/psum | solution.py:78
  (52 shorter events, 1.0 us)
Async XLA Ops:
  0.0 85.9 %copy-start = (bf16[3,4,64]{2,1,0:T(4,128)(2,1)S(1)}, bf16[3,4,64]{2,1,0:T(4,128)(2,1)}, u32[]{:S(2)}) copy-start(bf16[3,4,64]{2,1,0:T(4,128)(2,1)} %param.17) | copy-start | bytes 4612
  0.0 2.0 %copy-start.8 = (bf16[256,256]{1,0:T(8,128)(2,1)S(1)}, bf16[256,256]{1,0:T(8,128)(2,1)}, u32[]{:S(2)}) copy-start(bf16[256,256]{1,0:T(8,128)(2,1)} %param.12) | copy-start | bytes 393220
  1.9 0.9 copy-start.6
  1.9 1.6 %copy-start.10 = (s32[512]{0:T(512)S(1)}, s32[512]{0:T(512)}, u32[]{:S(2)}) copy-start(s32[512]{0:T(512)} %param.20) | copy-start | bytes 6148
  3.5 1.2 %copy-start.4 = (bf16[4,256,256]{2,1,0:T(8,128)(2,1)S(1)}, bf16[4,256,256]{2,1,0:T(8,128)(2,1)}, u32[]{:S(2)}) copy-start(bf16[4,256,256]{2,1,0:T(8,128)(2,1)} %param.11) | copy-start | bytes 1572868
  4.3 2.8 %copy-start.5 = (bf16[256,256]{1,0:T(8,128)(2,1)S(1)}, bf16[256,256]{1,0:T(8,128)(2,1)}, u32[]{:S(2)}) copy-start(bf16[256,256]{1,0:T(8,128)(2,1)} %param.13) | copy-start | bytes 393220
  4.7 2.4 %copy-start.3 = (bf16[4,256,256]{2,1,0:T(8,128)(2,1)S(1)}, bf16[4,256,256]{2,1,0:T(8,128)(2,1)}, u32[]{:S(2)}) copy-start(bf16[4,256,256]{2,1,0:T(8,128)(2,1)} %get-tuple-element.6) | copy-start | bytes 1572868
  4.7 2.4 %copy-start.7 = (bf16[256,256]{1,0:T(8,128)(2,1)S(1)}, bf16[256,256]{1,0:T(8,128)(2,1)}, u32[]{:S(2)}) copy-start(bf16[256,256]{1,0:T(8,128)(2,1)} %neg.3) | copy-start | bytes 393220
  6.6 0.5 copy-start.11
  25.3 10.4 %copy-start.9 = (s32[16]{0:T(128)S(1)}, s32[16]{0:T(128)}, u32[]{:S(2)}) copy-start(s32[16]{0:T(128)} %param.21) | copy-start | bytes 196
  25.3 21.4 %copy-start.1 = (s32[256]{0:T(256)S(1)}, s32[256]{0:T(256)}, u32[]{:S(2)}) copy-start(s32[256]{0:T(256)} %param.18) | copy-start | bytes 3076
  28.0 58.0 %all-to-all-start = ((bf16[4,512,256]{2,0,1:T(4,128)(2,1)}), bf16[4,512,256]{2,0,1:T(4,128)(2,1)S(1)}, u32[]{:S(2)}, u32[]{:S(2)}) async-start(bf16[4,512,256]{2,0,1:T(4,128)(2,1)} %select_bitcast_fusion), calls=%async_computation | async-start | bytes 2097152 | tf_op jit(solution)/shard_map/all_to_all | solution.py:54
  46.8 3.7 %copy-start.14 = (u32[32]{0:T(128)S(1)}, u32[32]{0:T(128)}, u32[]{:S(2)}) copy-start(u32[32]{0:T(128)} %constant.97) | copy-start | bytes 388
  46.8 4.9 %copy-start.12 = (f32[4]{0:T(128)S(1)}, f32[4]{0:T(128)}, u32[]{:S(2)}) copy-start(f32[4]{0:T(128)} %copy-done.11) | copy-start | bytes 52
  86.3 1.9 %copy-start.2 = (bf16[3,64,32,256]{3,2,1,0:T(8,128)(2,1)S(1)}, bf16[3,64,32,256]{3,2,1,0:T(8,128)(2,1)}, u32[]{:S(2)}) copy-start(bf16[3,64,32,256]{3,2,1,0:T(8,128)(2,1)} %param.16) | copy-start | bytes 9437188
  88.2 1.3 %copy-start.13 = (s32[4]{0:T(128)S(1)}, s32[4]{0:T(128)}, u32[]{:S(2)}) copy-start(s32[4]{0:T(128)} %param.19) | copy-start | bytes 52
where the time goes:
time: 120 us
  blocking collectives  64 us (53%)
  local copies, waits for them, and re-layouts  27.3 us (23%)
  other arithmetic  15 us (12%)
  starting transfers between devices  7.41 us (6%)
  matrix products  5.13 us (4%)
    unnamed x1, blocking collectives  33.9 us
    psum x1, blocking collectives, on_device(): return lax.psum(three_part - metric_part, 'aux')  30.1 us
    reshape x2, local copies, waits for them, and re-layouts, on_device(): triple.reshape(aux_local, tile_count, TILE, tile_count, TILE)  9.39 us
    all_to_all x1, starting transfers between devices, on_device(): lax.all_to_all(chosen, 'aux', split_axis=1, concat_axis=0, tiled=True)  7.41 us
    reshape x2, local copies, waits for them, and re-layouts, on_device(): blocked = blocked.reshape(aux_local, tile_count * tile_count, TILE * TILE)  5.89 us
    convert_element_type x1, other arithmetic, on_device(): (slot_ids % slot_depth < block_count[slot_ids // slot_depth]).astype(jnp....  5.67 us
    gather x10, other arithmetic, on_device(): block_count[slot_ids // slot_depth]  4.61 us
    gather x3, local copies, waits for them, and re-layouts, on_device(): function_atom[function_ids][:, :, None]  3.67 us
  transfers between devices with their start and end apart: 1, of which 0 were waited for; matrix products, arithmetic and copies ran while one was open for 13% of the time, Pallas kernels for 0%

commit v1 on v0

--- a/solution.py
+++ b/solution.py
@@ -51,7 +51,10 @@
     chosen = jnp.take(blocked, block_list, axis=1)
     slot_ids = jnp.arange(slot_total, dtype=jnp.int32)
     live_mask = (slot_ids % slot_depth < block_count[slot_ids // slot_depth]).astype(jnp.float32)
-    arrived = lax.all_to_all(chosen, "aux", split_axis=1, concat_axis=0, tiled=True)
+    devices = lax.axis_size("aux")
+    blocks = jnp.stack(jnp.split(chosen, devices, axis=1), axis=0)
+    blocks = lax.all_to_all(blocks, "aux", split_axis=0, concat_axis=0)
+    arrived = jnp.concatenate(blocks, axis=0)
     first_slot = lax.axis_index("aux") * slot_depth
     tile_ids = lax.dynamic_slice_in_dim(block_list, first_slot, slot_depth)
     slot_mask = lax.dynamic_slice_in_dim(live_mask, first_slot, slot_depth)

time: 120 us -> 130 us (1.083)
  local copies, waits for them, and re-layouts: 27.3 us -> 37.6 us
    unnamed x34 -> x49, local copies, waits for them, and re-layouts: 3.64 us -> 13.3 us
  transfers between devices with their start and end apart: 1 -> 1, of which waited for: 0 -> 0; matrix products, arithmetic and copies ran while one was open for 13% -> 12% of each run, Pallas kernels for 0% -> 0%
where the time goes in v1:
time: 130 us; the launch traced here: 129 us
  blocking collectives  64 us (49%)
  local copies, waits for them, and re-layouts  37.6 us (29%)
  other arithmetic  14.1 us (11%)
  starting transfers between devices  7.41 us (6%)
  matrix products  5.13 us (4%)
    unnamed x1, blocking collectives  33.9 us
    psum x1, blocking collectives, on_device(): return lax.psum(three_part - metric_part, 'aux')  30.1 us
    unnamed x49, local copies, waits for them, and re-layouts  13.3 us
    reshape x2, local copies, waits for them, and re-layouts, on_device(): triple.reshape(aux_local, tile_count, TILE, tile_count, TILE)  9.39 us
    all_to_all x1, starting transfers between devices, on_device(): blocks = lax.all_to_all(blocks, 'aux', split_axis=0, concat_axis=0)  7.41 us
    reshape x2, local copies, waits for them, and re-layouts, on_device(): blocked = blocked.reshape(aux_local, tile_count * tile_count, TILE * TILE)  5.89 us
    convert_element_type x1, other arithmetic, on_device(): (slot_ids % slot_depth < block_count[slot_ids // slot_depth]).astype(jnp....  5.67 us
    gather x10, other arithmetic, on_device(): block_count[slot_ids // slot_depth]  4.61 us
  transfers between devices with their start and end apart: 1, of which 0 were waited for; matrix products, arithmetic and copies ran while one was open for 12% of the time, Pallas kernels for 0%

profile of v1, /device:TPU:0, one launch (start us, length us, event | category | flops | bytes accessed | tf_op | source)
XLA Modules:
  0.0 129.1 jit_solution(2760419318186880401)
XLA Ops:
  0.0 1.8 %fusion = bf16[4,768,256]{2,1,0:T(8,128)(2,1)S(1)} fusion(bf16[4,256,256]{2,1,0:T(8,128)(2,1)} %param.11, bf16[256,256]{1,0:T(8,128)(2,1)} %param.15, bf16[256,256]{1,0:T(8,128)(2,1)} %param.14, bf16[256,256]{1,0:T(8,128)(2,1)} %param.13), kind=kOutput, calls=%fused_computation.5 | convolution fusion | flops 404619264 | bytes 2490368 | tf_op jit(solution)/shard_map/ab,pbc->pac/dot_general | solution.py:31
  2.8 0.7 neg.3
  3.7 0.9 slice_bitcast_fusion.1
  4.9 1.9 %convolution_bitcast_fusion.1 = f32[4]{0:T(128)S(1)} fusion(bf16[4,256,256]{2,1,0:T(8,128)(2,1)S(1)} %copy-done.4, bf16[256,256,1]{1,0,2:T(8,128)(2,1)} %bitcast.140), kind=kOutput, calls=%fused_computation.13 | convolution fusion | flops 524288 | bytes 655376 | tf_op jit(solution)/shard_map/pab,ab->p/dot_general | solution.py:29
  7.8 4.2 %reshape.111 = bf16[4,16,16,16,16]{4,3,2,1,0:T(8,128)(2,1)} reshape(bf16[4,256,256]{2,1,0:T(8,128)(2,1)S(1)} %fusion.3) | data formatting | bytes 1048576 | tf_op jit(solution)/shard_map/reshape | solution.py:49
  12.0 5.2 %copy.74 = bf16[4,16,16,16,16]{4,2,3,1,0:T(8,128)(2,1)} copy(bf16[4,16,16,16,16]{4,3,2,1,0:T(8,128)(2,1)} %reshape.111) | data formatting | bytes 1048576 | tf_op jit(solution)/shard_map/reshape | solution.py:49
  17.2 5.5 %reshape.112 = bf16[4,256,256]{2,1,0:T(8,128)(2,1)S(1)} reshape(bf16[4,16,16,16,16]{4,3,2,1,0:T(8,128)(2,1)} %bitcast.138) | data formatting | bytes 1048576 | tf_op jit(solution)/shard_map/reshape | solution.py:50
  23.1 2.4 %gather_fusion = bf16[512,4,256]{2,1,0:T(4,128)(2,1)S(1)} fusion(bf16[4,256,256]{2,0,1:T(4,128)(2,1)S(1)} %copy.44, s32[1024]{0:T(1024)S(1)} %get-tuple-element.24), kind=kCustom, calls=%fused_computation | custom fusion | bytes 2099200 | tf_op jit(solution)/shard_map/jit(_take)/gather | solution.py:51
  25.5 1.8 %select_bitcast_fusion = bf16[4,512,256]{2,0,1:T(4,128)(2,1)S(1)} fusion(bf16[512,4,256]{2,1,0:T(4,128)(2,1)S(1)} %gather_fusion, pred[512]{0:T(512)(128)(4,1)S(1)} %compare_and_fusion), kind=kLoop, calls=%fused_computation.18 | loop fusion | flops 524288 | bytes 2097664 | tf_op jit(solution)/shard_map/jit(_take)/select_n | solution.py:51
  27.4 0.6 fusion.34
  28.0 0.6 fusion.33
  28.6 0.6 fusion.32
  29.3 0.6 fusion.31
  29.9 0.6 fusion.30
  30.6 0.7 fusion.29
  31.2 0.6 fusion.28
  32.5 0.6 fusion.26
  33.1 0.6 fusion.25
  33.8 0.6 fusion.24
  34.4 0.6 fusion.23
  35.7 0.6 fusion.21
  36.3 0.6 fusion.20
  37.0 0.7 fusion.19
  37.6 7.4 %all-to-all-start = ((bf16[16,4,32,256]{3,1,2,0:T(4,128)(2,1)}), bf16[16,4,32,256]{3,1,2,0:T(4,128)(2,1)S(1)}, u32[]{:S(2)}, u32[]{:S(2)}) async-start(bf16[16,4,32,256]{3,1,2,0:T(4,128)(2,1)} %fusion.19), calls=%async_computation | async-start | bytes 2097152 | tf_op jit(solution)/shard_map/all_to_all | solution.py:56
  45.4 0.7 fusion.50
  46.1 4.3 %compare_select_fusion.2 = s32[512,1]{0,1:T(1,128)S(1)} fusion(s32[]{:T(128)} %bitcast.43, s32[]{:T(128)} %bitcast.44, s32[]{:T(128)} %bitcast.45, s32[]{:T(128)} %bitcast.46, s32[]{:T(128)} %bitcast.47, s32[]{:T(128)} %bitcast.49, s32[]{:T(128)} %bitcast.48), kind=kLoop, calls=%fused_computation.81 | loop fusion | flops 11776 | bytes 2076 | tf_op jit(solution)/shard_map/gather | solution.py:53
  50.4 5.7 %fusion.41 = f32[512]{0:T(512)S(1)} fusion(pred[512]{0:T(512)(128)(4,1)S(1)} %compare_reduce_fusion, pred[512]{0:T(512)(128)(4,1)S(1)} %compare_reduce_fusion.1, pred[512]{0:T(512)(128)(4,1)S(1)} %compare_reduce_fusion.2, pred[512]{0:T(512)(128)(4,1)S(1)} %compare_reduce_fusion.3, pred[512]{0:T(512)(128)(4,1)S(1)} %compare_reduce_fusion.4, ...), kind=kLoop, calls=%fused_computation.105 | loop fusion | flops 8704 | bytes 8740 | tf_op jit(solution)/shard_map/convert_element_type | solution.py:53
  56.2 3.5 %gather_fusion.1 = s32[512]{0:T(512)S(1)} fusion(s32[256]{0:T(256)S(1)} %copy-done.1, s32[1024]{0:T(1024)S(1)} %get-tuple-element.23), kind=kCustom, calls=%fused_computation.1 | custom fusion | bytes 6144 | tf_op jit(solution)/shard_map/gather | solution.py:70
  61.3 33.9 %all-reduce = f32[64]{0:T(128)S(1)} all-reduce(f32[64]{0:T(128)S(1)} %dynamic-update-slice), channel_id=1, replica_groups=mesh['grp'=2,'aux'=16] {'aux'}, use_global_device_ids=true, to_apply=%add | all-reduce | flops 64 | bytes 512
  96.0 1.5 %copy-done.2 = bf16[3,64,32,256]{3,2,1,0:T(8,128)(2,1)S(1)} copy-done((bf16[3,64,32,256]{3,2,1,0:T(8,128)(2,1)S(1)}, bf16[3,64,32,256]{3,2,1,0:T(8,128)(2,1)}, u32[]{:S(2)}) %copy-start.2) | copy-done | bytes 3145752
  97.6 0.7 multiply_reduce_fusion
  99.1 30.1 %psum.7 = f32[3,32]{1,0:T(4,128)} all-reduce(f32[3,32]{1,0:T(4,128)S(1)} %convolution_subtract_fusion), channel_id=1, replica_groups=mesh['grp'=2,'aux'=16] {'aux'}, use_global_device_ids=true, to_apply=%region_1.2 | all-reduce | flops 96 | bytes 768 | tf_op jit(solution)/shard_map/psum | solution.py:81
  (67 shorter events, 6.9 us)
Async XLA Ops:
  0.0 95.3 %copy-start = (bf16[3,4,64]{2,1,0:T(4,128)(2,1)S(1)}, bf16[3,4,64]{2,1,0:T(4,128)(2,1)}, u32[]{:S(2)}) copy-start(bf16[3,4,64]{2,1,0:T(4,128)(2,1)} %param.17) | copy-start | bytes 4612
  0.0 2.0 %copy-start.8 = (bf16[256,256]{1,0:T(8,128)(2,1)S(1)}, bf16[256,256]{1,0:T(8,128)(2,1)}, u32[]{:S(2)}) copy-start(bf16[256,256]{1,0:T(8,128)(2,1)} %param.12) | copy-start | bytes 393220
  1.9 0.9 copy-start.6
  1.9 1.6 %copy-start.10 = (s32[512]{0:T(512)S(1)}, s32[512]{0:T(512)}, u32[]{:S(2)}) copy-start(s32[512]{0:T(512)} %param.20) | copy-start | bytes 6148
  3.7 1.2 copy-start.4
  4.6 2.8 %copy-start.5 = (bf16[256,256]{1,0:T(8,128)(2,1)S(1)}, bf16[256,256]{1,0:T(8,128)(2,1)}, u32[]{:S(2)}) copy-start(bf16[256,256]{1,0:T(8,128)(2,1)} %param.13) | copy-start | bytes 393220
  4.9 2.4 %copy-start.3 = (bf16[4,256,256]{2,1,0:T(8,128)(2,1)S(1)}, bf16[4,256,256]{2,1,0:T(8,128)(2,1)}, u32[]{:S(2)}) copy-start(bf16[4,256,256]{2,1,0:T(8,128)(2,1)} %get-tuple-element.6) | copy-start | bytes 1572868
  4.9 2.4 %copy-start.7 = (bf16[256,256]{1,0:T(8,128)(2,1)S(1)}, bf16[256,256]{1,0:T(8,128)(2,1)}, u32[]{:S(2)}) copy-start(bf16[256,256]{1,0:T(8,128)(2,1)} %neg.3) | copy-start | bytes 393220
  6.8 0.5 copy-start.11
  27.3 18.0 %copy-start.9 = (s32[16]{0:T(128)S(1)}, s32[16]{0:T(128)}, u32[]{:S(2)}) copy-start(s32[16]{0:T(128)} %param.21) | copy-start | bytes 196
  28.0 28.2 %copy-start.1 = (s32[256]{0:T(256)S(1)}, s32[256]{0:T(256)}, u32[]{:S(2)}) copy-start(s32[256]{0:T(256)} %param.18) | copy-start | bytes 3076
  37.6 57.8 %all-to-all-start = ((bf16[16,4,32,256]{3,1,2,0:T(4,128)(2,1)}), bf16[16,4,32,256]{3,1,2,0:T(4,128)(2,1)S(1)}, u32[]{:S(2)}, u32[]{:S(2)}) async-start(bf16[16,4,32,256]{3,1,2,0:T(4,128)(2,1)} %fusion.19), calls=%async_computation | async-start | bytes 2097152 | tf_op jit(solution)/shard_map/all_to_all | solution.py:56
  56.2 3.7 %copy-start.14 = (u32[32]{0:T(128)S(1)}, u32[32]{0:T(128)}, u32[]{:S(2)}) copy-start(u32[32]{0:T(128)} %constant.97) | copy-start | bytes 388
  56.2 4.9 %copy-start.12 = (f32[4]{0:T(128)S(1)}, f32[4]{0:T(128)}, u32[]{:S(2)}) copy-start(f32[4]{0:T(128)} %copy-done.11) | copy-start | bytes 52
  95.7 1.9 %copy-start.2 = (bf16[3,64,32,256]{3,2,1,0:T(8,128)(2,1)S(1)}, bf16[3,64,32,256]{3,2,1,0:T(8,128)(2,1)}, u32[]{:S(2)}) copy-start(bf16[3,64,32,256]{3,2,1,0:T(8,128)(2,1)} %param.16) | copy-start | bytes 9437188
  97.5 1.3 %copy-start.13 = (s32[4]{0:T(128)S(1)}, s32[4]{0:T(128)}, u32[]{:S(2)}) copy-start(s32[4]{0:T(128)} %param.19) | copy-start | bytes 52
